TPU v7x, 32 devices: a whole 2x2x4 slice. The times are simulated.
32 devices in a mesh: blk: 2 (over x), tp: 4 (over z), qg: 4 (over y, core).
Axes of the slice: x: 2, y: 2, z: 4, core: 2. Of those that a mesh axis runs over, the one named last changes fastest.
Arguments:
- hidden_states: bfloat16 [1536, 4096], P(('blk', 'tp'), 'qg'), may hold values from -8 to 8
- query_states: bfloat16 [256, 4096], P('tp', 'qg'), may hold values from -8 to 8
- w_query: bfloat16 [4096, 4096], P('qg', 'tp'), may hold values from -0.25 to 0.25
- w_key: bfloat16 [4096, 1024], P('qg', 'tp'), may hold values from -0.09375 to 0.09375
- w_value: bfloat16 [4096, 1024], P('qg', 'tp'), may hold values from -0.09375 to 0.09375
- slot_order: int32 [4], replicated, may hold values from 0 to 3, each once
Outputs:
- attention: bfloat16 [1536, 4096], P(('blk', 'qg'), 'tp')
- decoded: bfloat16 [256, 4096], P('qg', 'tp')
Inputs may be any that keep to these rules, and one draw needn't show every extreme that they name: slot_order holds every number of 0 to 3 once.
All inputs are finite; a program needn't handle non-finite values.
Results may differ from a plain program's by a relative error of at most 0.00775.
The roundings to bfloat16 on the way count: a program that leaves them out, or rounds other values in their place, can miss the bound.
Values may be sent and summed in bfloat16 or wider, within the bound.
A program may use at most 128 MiB of HBM per device.

v0:
```python
import math
import jax
import jax.numpy as jnp
from jax import lax
from jax.sharding import PartitionSpec as P

HEAD_DIM = 128
rope_base = 500000.0
floor_value = -1e30


def slot_positions(slot_order, row_ids, span_len):
    slot_ids = jnp.arange(slot_order.shape[0], dtype=jnp.int32)
    picked = jnp.sum(
        jnp.where((row_ids // span_len)[:, None] == slot_ids[None, :], slot_order[None, :], 0),
        axis=1,
    )
    return picked * span_len + row_ids % span_len


def rotate(value_heads, position):
    full_dim = value_heads.shape[-1]
    half_dim = full_dim // 2
    frequency = jnp.float32(rope_base) ** (
        jnp.arange(half_dim, dtype=jnp.float32) * jnp.float32(-2.0 / full_dim)
    )
    angles = position[:, None] * frequency[None, :]
    cosine = jnp.cos(angles)[:, None, :]
    sine_table = jnp.sin(angles)[:, None, :]
    front_half = value_heads[..., :half_dim]
    back_half = value_heads[..., half_dim:]
    return jnp.concatenate(
        [
            front_half * cosine - back_half * sine_table,
            back_half * cosine + front_half * sine_table,
        ],
        axis=-1,
    )


def heads_first(queries, kv_heads, sharing):
    row_count = queries.shape[0]
    shaped = queries.reshape(row_count, kv_heads, sharing, queries.shape[-1])
    return jnp.transpose(shaped, (1, 0, 2, 3)).reshape(
        kv_heads, row_count * sharing, queries.shape[-1]
    )


def empty_state(kv_heads, row_count, head_dim):
    return (
        jnp.full((kv_heads, row_count), floor_value, jnp.float32),
        jnp.zeros((kv_heads, row_count), jnp.float32),
        jnp.zeros((kv_heads, row_count, head_dim), jnp.float32),
    )


def block_update(carried, queries, key_heads, value_heads, allowed):
    running_max, normalizer, weighted = carried
    scaling = 1.0 / math.sqrt(queries.shape[-1])
    scores = (
        jnp.einsum("gqd,kgd->gqk", queries, key_heads, preferred_element_type=jnp.float32) * scaling
    )
    if allowed is not None:
        scores = jnp.where(allowed[None, :, :], scores, -jnp.inf)
    new_max = jnp.maximum(running_max, jnp.max(scores, axis=-1))
    weights = jnp.exp(scores - new_max[..., None])
    shrink = jnp.exp(running_max - new_max)
    normalizer = normalizer * shrink + jnp.sum(weights, axis=-1)
    product = jnp.einsum(
        "gqk,kgd->gqd",
        weights.astype(jnp.bfloat16),
        value_heads,
        preferred_element_type=jnp.float32,
    )
    return (new_max, normalizer, weighted * shrink[..., None] + product)


def key_step(row_count, shard_rows):
    chosen = shard_rows
    factor = 2
    while shard_rows * factor <= 1024 and shard_rows * factor <= row_count:
        if row_count % (shard_rows * factor) == 0:
            chosen = shard_rows * factor
        factor = factor + 1
    return chosen


def run_blocks(
    carried, pieces, first_row, queries, query_pos, slot_order, span_len, shard_rows, masked
):
    row_count = pieces.shape[0]
    block_len = key_step(row_count, shard_rows)
    kv_cols = pieces.shape[1] // 2
    kv_heads = queries.shape[0]
    head_dim = queries.shape[2]
    first_row = jnp.asarray(first_row)

    def one_block(turn_index, inner_state):
        offset = turn_index * block_len
        key_block = lax.dynamic_slice_in_dim(pieces, offset, block_len, 0)
        key_heads = key_block[:, :kv_cols].reshape(block_len, kv_heads, head_dim)
        value_heads = key_block[:, kv_cols:].reshape(block_len, kv_heads, head_dim)
        if not masked:
            return block_update(inner_state, queries, key_heads, value_heads, None)
        key_pos = slot_positions(
            slot_order, offset + jnp.arange(block_len, dtype=jnp.int32), span_len
        )
        allowed = key_pos[None, :] <= query_pos[:, None]
        return block_update(inner_state, queries, key_heads, value_heads, allowed)

    return lax.fori_loop(0, row_count // block_len, one_block, carried)


def finish(carried, row_count, sharing):
    running_max, normalizer, weighted = carried
    kv_heads = weighted.shape[0]
    head_dim = weighted.shape[2]
    result = (weighted / normalizer[..., None]).reshape(kv_heads, row_count, sharing, head_dim)
    return (
        jnp.transpose(result, (1, 0, 2, 3))
        .reshape(row_count, kv_heads * sharing * head_dim)
        .astype(jnp.bfloat16)
    )


def body(hidden_states, query_states, w_query, w_key, w_value, slot_order):
    block_rows, query_rows = (
        lax.all_gather(hidden_states, "tp", axis=0, tiled=True),
        lax.all_gather(query_states, "tp", axis=0, tiled=True),
    )
    qg_count = lax.axis_size("qg")
    member = lax.axis_index("qg")
    blk_index = lax.axis_index("blk")
    head_dim = HEAD_DIM
    heads_local = w_query.shape[1] // head_dim
    kv_heads = w_key.shape[1] // head_dim
    sharing = heads_local // kv_heads
    kv_cols = w_key.shape[1]
    group_rows = block_rows.shape[0]
    span_len = group_rows // 2
    own_rows = group_rows // qg_count
    own_queries = query_rows.shape[0] // qg_count
    columns = block_rows.shape[1]
    seq_len = group_rows * lax.axis_size("blk")
    stacked = jnp.concatenate(
        [
            block_rows.reshape(qg_count, own_rows, columns),
            query_rows.reshape(qg_count, own_queries, columns),
        ],
        axis=1,
    ).reshape(qg_count * (own_rows + own_queries), columns)
    query_sum = lax.psum_scatter(
        jnp.dot(stacked, w_query, preferred_element_type=jnp.float32),
        "qg",
        scatter_dimension=0,
        tiled=True,
    )
    partial_value = jnp.dot(
        block_rows, jnp.concatenate([w_key, w_value], axis=1), preferred_element_type=jnp.float32
    )
    kv_sum = lax.psum(partial_value, "qg")
    kv_start = blk_index * group_rows
    kv_rows = kv_sum.shape[0]
    key_pos = slot_positions(slot_order, kv_start + jnp.arange(kv_rows, dtype=jnp.int32), span_len)
    key_heads = rotate(
        kv_sum[:, :kv_cols].reshape(kv_rows, kv_heads, head_dim), key_pos.astype(jnp.float32)
    )
    kv_cache = jnp.concatenate(
        [
            key_heads.reshape(kv_rows, kv_cols).astype(jnp.bfloat16),
            kv_sum[:, kv_cols:].astype(jnp.bfloat16),
        ],
        axis=1,
    )
    query_start = blk_index * group_rows + member * own_rows
    query_pos = slot_positions(
        slot_order, query_start + jnp.arange(own_rows, dtype=jnp.int32), span_len
    )
    queries = rotate(
        query_sum[:own_rows].reshape(own_rows, heads_local, head_dim), query_pos.astype(jnp.float32)
    ).astype(jnp.bfloat16)
    queries = heads_first(queries, kv_heads, sharing)
    repeated = jnp.repeat(query_pos, sharing)
    fresh_pos = jnp.full((own_queries,), seq_len, jnp.float32)
    decode_query = rotate(
        query_sum[own_rows:].reshape(own_queries, heads_local, head_dim), fresh_pos
    ).astype(jnp.bfloat16)
    asked = heads_first(decode_query, kv_heads, sharing)
    starting = (
        empty_state(kv_heads, own_rows * sharing, head_dim),
        empty_state(kv_heads, own_queries * sharing, head_dim),
    )
    pieces = lax.all_gather(kv_cache, "blk", axis=0, tiled=True)
    first_row = jnp.int32(0)
    prefill_state = run_blocks(
        starting[0], pieces, first_row, queries, repeated, slot_order, span_len, kv_rows, True
    )
    decode_state = run_blocks(
        starting[1], pieces, first_row, asked, None, slot_order, span_len, kv_rows, False
    )
    carried, decode_state = (prefill_state, decode_state)
    decoded = finish(decode_state, own_queries, sharing)
    attention = finish(carried, own_rows, sharing)
    return (attention, decoded)


def solution(mesh):
    return jax.shard_map(
        body,
        mesh=mesh,
        in_specs=(
            P(("blk", "tp"), "qg"),
            P("tp", "qg"),
            P("qg", "tp"),
            P("qg", "tp"),
            P("qg", "tp"),
            P(),
        ),
        out_specs=(P(("blk", "qg"), "tp"), P("qg", "tp")),
        check_vma=False,
    )
```

profile of v0, /device:TPU:0, one launch (start us, length us, event | category | flops | bytes accessed | tf_op | source)
XLA Modules:
  0.0 200.1 jit_solution(10457108261832202985)
XLA Ops:
  7.2 0.7 all-gather.3.cloned.1.call-update
  8.0 41.4 %all-gather.3.cloned.1.call-done = bf16[768,1024]{1,0:T(8,128)(2,1)} async-done(((bf16[192,1024]{1,0:T(8,128)(2,1)}), bf16[768,1024]{1,0:T(8,128)(2,1)}) %all-gather.3.cloned.1.call-update) | async-done | bytes 1572880 | tf_op jit(solution)/shard_map/all_gather | solution.py:128
  49.3 3.9 %convolution_bitcast_fusion = f32[768,512]{0,1:T(8,128)} fusion(bf16[768,1024]{1,0:T(8,128)(2,1)} %all-gather.3.cloned.1.call-done, bf16[1024,256]{1,0:T(8,128)(2,1)} %param.14, bf16[1024,256]{1,0:T(8,128)(2,1)} %param.13), kind=kOutput, calls=%fused_computation.47 | convolution fusion | flops 807403520 | bytes 4194304 | tf_op jit(solution)/shard_map/dot_general | solution.py:158
  53.4 15.9 %all_gather.11 = bf16[256,1024]{1,0:T(8,128)(2,1)S(1)} all-gather(bf16[64,1024]{1,0:T(8,128)(2,1)S(1)} %copy-done.3), channel_id=1, replica_groups=mesh['blk'=2,'tp'=4,'qg'=4] {'tp'}, dimensions={0}, use_global_device_ids=true | all-gather | bytes 655360 | tf_op jit(solution)/shard_map/all_gather | solution.py:129
  69.3 1.7 pad_maximum_fusion
  71.0 4.3 %fusion.46 = f32[1024,1024]{1,0:T(8,128)} fusion(bf16[1024,1024]{1,0:T(8,128)(2,1)S(1)} %bitcast.106, bf16[1024,1024]{1,0:T(8,128)(2,1)S(1)} %copy-done), kind=kOutput, calls=%fused_computation.100 | convolution fusion | flops 2147483648 | bytes 8388608 | tf_op jit(solution)/shard_map/dot_general | solution.py:153
  76.1 0.8 multiply_cosine_fusion
  76.9 18.3 %all-reduce.2.cloned.1.call-done = f32[768,512]{0,1:T(8,128)} async-done(((f32[768,512]{0,1:T(8,128)}), f32[768,512]{0,1:T(8,128)}) %all-reduce.2.cloned.1.call-update) | async-done | bytes 1572880 | tf_op jit(solution)/shard_map/psum | solution.py:161
  95.2 1.2 slice.104
  96.7 0.9 pad_maximum_fusion.1
  98.2 44.2 %reduce-scatter.2.cloned.1.call-done = f32[256,1024]{1,0:T(8,128)} async-done(((f32[1024,1024]{1,0:T(8,128)}), f32[256,1024]{1,0:T(8,128)}) %reduce-scatter.2.cloned.1.call-update) | async-done | bytes 1048592 | tf_op jit(solution)/shard_map/reduce_scatter | solution.py:152
  142.4 1.2 slice_bitcast_fusion
  144.2 0.5 pad_maximum_fusion.3
  144.9 1.0 slice_bitcast_fusion.1
  146.3 24.7 %all-gather.5.cloned.1.call-done = bf16[1536,512]{0,1:T(8,128)(2,1)} async-done(((bf16[768,512]{0,1:T(8,128)(2,1)}), bf16[1536,512]{0,1:T(8,128)(2,1)}) %all-gather.5.cloned.1.call-update) | async-done | bytes 1572880 | tf_op jit(solution)/shard_map/all_gather | solution.py:193
  171.0 4.8 %while.39 = (s32[]{:T(128)}, f32[2,256]{1,0:T(2,128)S(1)}, f32[2,256]{1,0:T(2,128)S(1)}, f32[2,256,128]{2,1,0:T(8,128)S(1)}, bf16[1536,512]{0,1:T(8,128)(2,1)}, ...) while((s32[]{:T(128)}, f32[2,256]{1,0:T(2,128)S(1)}, ...), condition=%wide.region_12.13_spmd.clone, body=%wide.region_9.12_spmd.clone.sunk | while | flops 203885056 | bytes 7766211 | solution.py:111
  171.0 1.2 fusion.90
  173.4 1.2 fusion.90
  176.0 0.7 convert_element_type.74
  176.8 14.2 %while.38 = (s32[]{:T(128)}, f32[2,768]{1,0:T(2,128)S(1)}, f32[2,768]{1,0:T(2,128)S(1)}, f32[2,768,128]{2,1,0:T(8,128)}, s32[4]{0:T(128)S(1)}, /*index=5*/bf16[1...) while((s32[]{:T(128)}, f32[2,768]{1,0:T(2,128)S(1)}, ...), condition=%wide.region_8.9_spmd.clone, body=%wide.region_4.8_spmd.clone.sunk | while | flops 618165504 | bytes 27261984 | solution.py:111
  177.5 1.2 fusion.80
  178.7 1.2 fusion.81
  179.9 1.1 fusion.83
  181.0 1.9 fusion.85
  182.9 0.9 copy-done.2
  184.6 1.2 fusion.80
  185.8 1.2 fusion.81
  187.0 1.1 fusion.83
  188.1 1.9 fusion.85
  190.0 0.9 copy-done.2
  191.0 1.4 divide_convert_fusion
  192.5 1.0 convert_element_type.70
  (78 shorter events, 7.0 us)
Async XLA Ops:
  7.2 63.8 %copy-start = (bf16[1024,1024]{1,0:T(8,128)(2,1)S(1)}, bf16[1024,1024]{1,0:T(8,128)(2,1)}, u32[]{:S(2)}) copy-start(bf16[1024,1024]{1,0:T(8,128)(2,1)} %param.12) | copy-start | bytes 6291460
  7.2 42.2 %all-gather.3.cloned.1.call-start = ((), (), s32[]{:S(2)}) async-start(), calls=%async_computation.1 | async-start | bytes 1966080 | tf_op jit(solution)/shard_map/all_gather | solution.py:128
  7.9 45.4 %copy-start.3 = (bf16[64,1024]{1,0:T(8,128)(2,1)S(1)}, bf16[64,1024]{1,0:T(8,128)(2,1)}, u32[]{:S(2)}) copy-start(bf16[64,1024]{1,0:T(8,128)(2,1)} %param.11) | copy-start | bytes 393220
  7.9 87.3 %all-reduce.2.cloned.1.call-start = ((), (), s32[]{:S(2)}) async-start(), calls=%async_computation.2 | async-start | bytes 3145728 | tf_op jit(solution)/shard_map/psum | solution.py:161
  53.3 89.1 %reduce-scatter.2.cloned.1.call-start = ((), (), s32[]{:S(2)}) async-start(), calls=%async_computation.4 | async-start | bytes 5242880 | tf_op jit(solution)/shard_map/reduce_scatter | solution.py:152
  75.2 0.7 copy-start.4
  75.3 95.7 %all-gather.5.cloned.1.call-start = ((), (), s32[]{:S(2)}) async-start(), calls=%async_computation.3 | async-start | bytes 2359296 | tf_op jit(solution)/shard_map/all_gather | solution.py:193
  95.2 1.4 slice-start
  179.9 1.1 copy-start.1
  182.9 0.9 copy-start.2
  187.0 1.1 copy-start.1
  190.0 0.9 copy-start.2
Sparse Core Ops, SparseCore 0:
  9.6 39.7 all-gather.2
  53.4 41.7 all-reduce.1
  97.7 44.6 reduce-scatter.1
  143.8 27.1 all-gather.4
where the time goes:
time: 201 us; the launch traced here: 200 us
  waiting for transfers between devices  129 us (64%)
  matrix products  16.3 us (8%)
  blocking collectives  15.9 us (8%)
  between operations  14 us (7%)
  local copies, waits for them, and re-layouts  13.1 us (7%)
  other arithmetic  10.8 us (5%)
    reduce_scatter x1, waiting for transfers between devices, body(): lax.psum_scatter(jnp.dot(stacked, w_query, preferred_element_type=jnp.flo...  44.2 us
    all_gather x1, waiting for transfers between devices, body(): lax.all_gather(hidden_states, 'tp', axis=0, tiled=True)  41.4 us
    all_gather x1, waiting for transfers between devices, body(): pieces = lax.all_gather(kv_cache, 'blk', axis=0, tiled=True)  24.7 us
    psum x1, waiting for transfers between devices, body(): kv_sum = lax.psum(partial_value, 'qg')  18.3 us
    all_gather x1, blocking collectives, body(): lax.all_gather(query_states, 'tp', axis=0, tiled=True)  15.9 us
    dot_general x4, matrix products, block_update(): jnp.einsum('gqk,kgd->gqd', weights.astype(jnp.bfloat16), value_heads, pre...  4.86 us
    slice x4, local copies, waits for them, and re-layouts, one_block(): value_heads = key_block[:, kv_cols:].reshape(block_len, kv_heads, head_dim)  4.69 us
    dot_general x1, matrix products, body(): jnp.dot(stacked, w_query, preferred_element_type=jnp.float32)  4.29 us
  transfers between devices with their start and end apart: 4, of which 4 were waited for; matrix products, arithmetic and copies ran while one was open for 7% of the time, Pallas kernels for 0%

commit v1 on v0

--- a/solution.py
+++ b/solution.py
@@ -158,7 +158,7 @@
     partial_value = jnp.dot(
         block_rows, jnp.concatenate([w_key, w_value], axis=1), preferred_element_type=jnp.float32
     )
-    kv_sum = lax.psum(partial_value, "qg")
+    kv_sum = jnp.sum(lax.all_gather(partial_value, "qg"), axis=0)
     kv_start = blk_index * group_rows
     kv_rows = kv_sum.shape[0]
     key_pos = slot_positions(slot_order, kv_start + jnp.arange(kv_rows, dtype=jnp.int32), span_len)

time: 201 us -> 221 us (1.100)
  other arithmetic: 10.8 us -> 27.2 us
  waiting for transfers between devices: 129 us -> 115 us
  local copies, waits for them, and re-layouts: 13.1 us -> 22.4 us
  matrix products: 16.3 us -> 25.4 us
    all_gather x0 -> x1, waiting for transfers between devices: none -> 21.8 us  [body(): kv_sum = jnp.sum(lax.all_gather(partial_value, 'qg'), axis=0)]
    psum x1 -> x0, waiting for transfers between devices: 18.3 us -> none  [body(): kv_sum = lax.psum(partial_value, 'qg')]
    reduce_scatter x1, waiting for transfers between devices: 44.2 us -> 27.5 us  [body(): lax.psum_scatter(jnp.dot(stacked, w_query, preferred_element_type=jnp.flo...]
    reduce_sum x0 -> x1, other arithmetic: none -> 8.39 us  [body(): kv_sum = jnp.sum(lax.all_gather(partial_value, 'qg'), axis=0)]
    all_gather x0 -> x1, local copies, waits for them, and re-layouts: none -> 8.3 us  [body(): kv_sum = jnp.sum(lax.all_gather(partial_value, 'qg'), axis=0)]
    reduce_sum x4, other arithmetic: 2.63 us -> 10.7 us  [block_update(): normalizer = normalizer * shrink + jnp.sum(weights, axis=-1)]
    dot_general x4, matrix products: 3.22 us -> 9.63 us  [block_update(): jnp.einsum('gqd,kgd->gqk', queries, key_heads, preferred_element_type=jnp...]
    dot_general x4, matrix products: 4.86 us -> 7.53 us  [block_update(): jnp.einsum('gqk,kgd->gqd', weights.astype(jnp.bfloat16), value_heads, pre...]
  transfers between devices with their start and end apart: 4 -> 4, of which waited for: 4 -> 4; matrix products, arithmetic and copies ran while one was open for 7% -> 14% of each run, Pallas kernels for 0% -> 0%
where the time goes in v1:
time: 221 us
  waiting for transfers between devices  115 us (52%)
  other arithmetic  27.2 us (12%)
  matrix products  25.4 us (11%)
  local copies, waits for them, and re-layouts  22.4 us (10%)
  blocking collectives  15.9 us (7%)
  between operations  14 us (6%)
    all_gather x1, waiting for transfers between devices, body(): lax.all_gather(hidden_states, 'tp', axis=0, tiled=True)  41.4 us
    reduce_scatter x1, waiting for transfers between devices, body(): lax.psum_scatter(jnp.dot(stacked, w_query, preferred_element_type=jnp.flo...  27.5 us
    all_gather x1, waiting for transfers between devices, body(): pieces = lax.all_gather(kv_cache, 'blk', axis=0, tiled=True)  24.1 us
    all_gather x1, waiting for transfers between devices, body(): kv_sum = jnp.sum(lax.all_gather(partial_value, 'qg'), axis=0)  21.8 us
    all_gather x1, blocking collectives, body(): lax.all_gather(query_states, 'tp', axis=0, tiled=True)  15.9 us
    reduce_sum x4, other arithmetic, block_update(): normalizer = normalizer * shrink + jnp.sum(weights, axis=-1)  10.7 us
    dot_general x4, matrix products, block_update(): jnp.einsum('gqd,kgd->gqk', queries, key_heads, preferred_element_type=jnp...  9.63 us
    reduce_sum x1, other arithmetic, body(): kv_sum = jnp.sum(lax.all_gather(partial_value, 'qg'), axis=0)  8.39 us
  transfers between devices with their start and end apart: 4, of which 4 were waited for; matrix products, arithmetic and copies ran while one was open for 14% of the time, Pallas kernels for 0%

profile of v1, /device:TPU:0, one launch (start us, length us, event | category | flops | bytes accessed | tf_op | source)
XLA Modules:
  0.0 220.8 jit_solution(8134922366220937164)
XLA Ops:
  8.0 41.4 %all-gather.5.cloned.1.call-done = bf16[768,1024]{1,0:T(8,128)(2,1)} async-done(((bf16[192,1024]{1,0:T(8,128)(2,1)}), bf16[768,1024]{1,0:T(8,128)(2,1)}) %all-gather.5.cloned.1.call-update) | async-done | bytes 1572880 | tf_op jit(solution)/shard_map/all_gather | solution.py:128
  49.3 3.9 %convolution_bitcast_fusion = f32[768,512]{0,1:T(8,128)} fusion(bf16[768,1024]{1,0:T(8,128)(2,1)} %all-gather.5.cloned.1.call-done, bf16[1024,256]{1,0:T(8,128)(2,1)} %param.14, bf16[1024,256]{1,0:T(8,128)(2,1)} %param.13), kind=kOutput, calls=%fused_computation.47 | convolution fusion | flops 807403520 | bytes 4194304 | tf_op jit(solution)/shard_map/dot_general | solution.py:158
  53.3 15.9 %all_gather.19 = bf16[256,1024]{1,0:T(8,128)(2,1)S(1)} all-gather(bf16[64,1024]{1,0:T(8,128)(2,1)S(1)} %copy-done.6), channel_id=1, replica_groups=mesh['blk'=2,'tp'=4,'qg'=4] {'tp'}, dimensions={0}, use_global_device_ids=true | all-gather | bytes 655360 | tf_op jit(solution)/shard_map/all_gather | solution.py:129
  69.3 1.7 pad_maximum_fusion
  70.9 4.3 %fusion.46 = f32[1024,1024]{1,0:T(8,128)} fusion(bf16[1024,1024]{1,0:T(8,128)(2,1)S(1)} %bitcast.108, bf16[1024,1024]{1,0:T(8,128)(2,1)S(1)} %copy-done), kind=kOutput, calls=%fused_computation.100 | convolution fusion | flops 2147483648 | bytes 8388608 | tf_op jit(solution)/shard_map/dot_general | solution.py:153
  76.9 21.8 %all-gather.9.cloned.1.call-done = f32[3072,512]{0,1:T(8,128)} async-done(((f32[768,512]{0,1:T(8,128)}), f32[3072,512]{0,1:T(8,128)}) %all-gather.9.cloned.1.call-update) | async-done | bytes 6291472 | tf_op jit(solution)/shard_map/all_gather | solution.py:161
  98.7 8.3 %reshape.311 = f32[4,768,512]{1,0,2:T(4,128)} reshape(f32[3072,512]{0,1:T(8,128)} %all-gather.9.cloned.1.call-done) | data formatting | bytes 12582912 | tf_op jit(solution)/shard_map/all_gather | solution.py:161
  107.0 8.4 %reduce_sum.73 = f32[768,512]{0,1:T(8,128)} reduce(f32[4,768,512]{1,0,2:T(4,128)} %reshape.311, f32[]{:T(128)} %constant.189.clone.1), dimensions={0}, to_apply=%region_0.0 | reduce | flops 1179648 | bytes 7864324 | tf_op jit(solution)/shard_map/reduce_sum | solution.py:161
  115.4 1.2 slice.104
  116.9 0.9 pad_maximum_fusion.1
  118.3 27.5 %reduce-scatter.2.cloned.1.call-done = f32[256,1024]{1,0:T(8,128)} async-done(((f32[1024,1024]{1,0:T(8,128)}), f32[256,1024]{1,0:T(8,128)}) %reduce-scatter.2.cloned.1.call-update) | async-done | bytes 1048592 | tf_op jit(solution)/shard_map/reduce_scatter | solution.py:152
  145.8 1.2 slice_bitcast_fusion
  148.3 1.0 slice_bitcast_fusion.1
  150.3 24.1 %all-gather.7.cloned.1.call-done = bf16[1536,512]{0,1:T(8,128)(2,1)} async-done(((bf16[768,512]{0,1:T(8,128)(2,1)}), bf16[1536,512]{0,1:T(8,128)(2,1)}) %all-gather.7.cloned.1.call-update) | async-done | bytes 1572880 | tf_op jit(solution)/shard_map/all_gather | solution.py:193
  174.4 26.0 %while.38 = (s32[]{:T(128)}, f32[2,768]{1,0:T(2,128)S(1)}, f32[2,768]{1,0:T(2,128)S(1)}, f32[2,768,128]{2,1,0:T(8,128)}, s32[4]{0:T(128)S(1)}, /*index=5*/bf16[1...) while((s32[]{:T(128)}, f32[2,768]{1,0:T(2,128)S(1)}, ...), condition=%wide.region_8.9_spmd.clone, body=%wide.region_4.8_spmd.clone.sunk | while | flops 618165504 | bytes 41417752 | solution.py:111
  174.4 1.9 fusion.80
  177.1 3.2 %fusion.81 = (f32[2,768]{1,0:T(2,128)S(1)}, f32[2,768,768]{2,1,0:T(8,128)}) fusion(pred[768,768]{0,1:T(8,128)(4,1)S(1)} %broadcast_compare_fusion.2, bf16[768,2,128]{0,2,1:T(8,128)(2,1)S(1)} %bitcast.99, bf16[2,768,128]{2,1,0:T(8,128)(2,1)S(1)} %get-tuple-element.565), kind=kOutput, calls=%fused_computation.5.clone.1 | convolution fusion | flops 305527296 | bytes 6100992 | tf_op jit(solution)/shard_map/while/body/eval_jaxpr/gqd,kgd->gqk/dot_general | solution.py:61
  180.3 3.6 %fusion.83 = f32[2,768]{1,0:T(2,128)S(1)} fusion(f32[2,768,768]{2,1,0:T(8,128)} %get-tuple-element.517, f32[2,768]{1,0:T(2,128)S(1)} %fusion.82, pred[768,768]{0,1:T(8,128)(4,1)S(1)} %broadcast_compare_fusion.2), kind=kLoop, calls=%fused_computation.4.clone.1 | loop fusion | flops 4717056 | bytes 5320704 | tf_op jit(solution)/shard_map/while/body/eval_jaxpr/reduce_sum | solution.py:68
  184.1 2.7 %fusion.85 = f32[2,768,128]{2,1,0:T(8,128)} fusion(bf16[768,2,128]{0,2,1:T(8,128)(2,1)S(1)} %bitcast.103, f32[2,768,768]{2,1,0:T(8,128)S(1)} %copy-done.1, f32[2,768]{1,0:T(2,128)S(1)} %fusion.82, pred[768,768]{0,1:T(8,128)(4,1)S(1)} %broadcast_compare_fusion.2, f32[2,768,128]{2,1,0:T(8,128)} %get-tuple-element.549, ...), kind=kOutput, calls=%fused_computation.8.clone.1 | convolution fusion | flops 307298304 | bytes 7286785 | tf_op jit(solution)/shard_map/while/body/eval_jaxpr/gqk,kgd->gqd/dot_general | solution.py:69
  186.8 1.9 fusion.80
  189.5 3.2 %fusion.81 = (f32[2,768]{1,0:T(2,128)S(1)}, f32[2,768,768]{2,1,0:T(8,128)}) fusion(pred[768,768]{0,1:T(8,128)(4,1)S(1)} %broadcast_compare_fusion.2, bf16[768,2,128]{0,2,1:T(8,128)(2,1)S(1)} %bitcast.99, bf16[2,768,128]{2,1,0:T(8,128)(2,1)S(1)} %get-tuple-element.565), kind=kOutput, calls=%fused_computation.5.clone.1 | convolution fusion | flops 305527296 | bytes 6100992 | tf_op jit(solution)/shard_map/while/body/eval_jaxpr/gqd,kgd->gqk/dot_general | solution.py:61
  192.7 3.6 %fusion.83 = f32[2,768]{1,0:T(2,128)S(1)} fusion(f32[2,768,768]{2,1,0:T(8,128)} %get-tuple-element.517, f32[2,768]{1,0:T(2,128)S(1)} %fusion.82, pred[768,768]{0,1:T(8,128)(4,1)S(1)} %broadcast_compare_fusion.2), kind=kLoop, calls=%fused_computation.4.clone.1 | loop fusion | flops 4717056 | bytes 5320704 | tf_op jit(solution)/shard_map/while/body/eval_jaxpr/reduce_sum | solution.py:68
  196.6 3.8 %fusion.85 = f32[2,768,128]{2,1,0:T(8,128)} fusion(bf16[768,2,128]{0,2,1:T(8,128)(2,1)S(1)} %bitcast.103, f32[2,768,768]{2,1,0:T(8,128)S(1)} %copy-done.1, f32[2,768]{1,0:T(2,128)S(1)} %fusion.82, pred[768,768]{0,1:T(8,128)(4,1)S(1)} %broadcast_compare_fusion.2, f32[2,768,128]{2,1,0:T(8,128)} %get-tuple-element.549, ...), kind=kOutput, calls=%fused_computation.8.clone.1 | convolution fusion | flops 307298304 | bytes 7286785 | tf_op jit(solution)/shard_map/while/body/eval_jaxpr/gqk,kgd->gqd/dot_general | solution.py:69
  200.4 1.5 divide_convert_fusion
  202.0 1.0 convert_element_type.70
  203.0 10.3 %while.39 = (s32[]{:T(128)}, f32[2,256]{1,0:T(2,128)S(1)}, f32[2,256]{1,0:T(2,128)S(1)}, f32[2,256,128]{2,1,0:T(8,128)S(1)}, bf16[1536,512]{0,1:T(8,128)(2,1)}, ...) while((s32[]{:T(128)}, f32[2,256]{1,0:T(2,128)S(1)}, ...), condition=%wide.region_12.13_spmd.clone, body=%wide.region_9.12_spmd.clone.sunk | while | flops 203885056 | bytes 14057687 | solution.py:111
  203.0 1.2 fusion.90
  204.2 1.6 bitcast_reduce_fusion.2
  205.8 1.8 fusion.92
  208.2 1.2 fusion.90
  209.3 1.6 bitcast_reduce_fusion.2
  210.9 1.8 fusion.92
  (88 shorter events, 9.6 us)
Async XLA Ops:
  7.2 63.8 %copy-start = (bf16[1024,1024]{1,0:T(8,128)(2,1)S(1)}, bf16[1024,1024]{1,0:T(8,128)(2,1)}, u32[]{:S(2)}) copy-start(bf16[1024,1024]{1,0:T(8,128)(2,1)} %param.12) | copy-start | bytes 6291460
  7.2 42.2 %all-gather.5.cloned.1.call-start = ((), (), s32[]{:S(2)}) async-start(), calls=%async_computation.1 | async-start | bytes 1966080 | tf_op jit(solution)/shard_map/all_gather | solution.py:128
  7.9 45.4 %copy-start.6 = (bf16[64,1024]{1,0:T(8,128)(2,1)S(1)}, bf16[64,1024]{1,0:T(8,128)(2,1)}, u32[]{:S(2)}) copy-start(bf16[64,1024]{1,0:T(8,128)(2,1)} %param.11) | copy-start | bytes 393220
  7.9 90.7 %all-gather.9.cloned.1.call-start = ((), (), s32[]{:S(2)}) async-start(), calls=%async_computation.4 | async-start | bytes 7864320 | tf_op jit(solution)/shard_map/all_gather | solution.py:161
  53.3 92.5 %reduce-scatter.2.cloned.1.call-start = ((), (), s32[]{:S(2)}) async-start(), calls=%async_computation.3 | async-start | bytes 5242880 | tf_op jit(solution)/shard_map/reduce_scatter | solution.py:152
  75.2 0.7 copy-start.7
  75.3 99.2 %all-gather.7.cloned.1.call-start = ((), (), s32[]{:S(2)}) async-start(), calls=%async_computation.2 | async-start | bytes 2359296 | tf_op jit(solution)/shard_map/all_gather | solution.py:193
  115.4 1.4 slice-start
  180.3 3.8 %copy-start.1 = (f32[2,768,768]{2,1,0:T(8,128)S(1)}, f32[2,768,768]{2,1,0:T(8,128)}, u32[]{:S(2)}) copy-start(f32[2,768,768]{2,1,0:T(8,128)} %get-tuple-element.517) | copy-start | bytes 14155780 | tf_op jit(solution)/shard_map/while
  180.3 3.8 %copy-start.3 = (bf16[768,256]{0,1:T(8,128)(2,1)S(1)}, bf16[768,256]{0,1:T(8,128)(2,1)}, u32[]{:S(2)}) copy-start(bf16[768,256]{0,1:T(8,128)(2,1)} %get-tuple-element.519) | copy-start | bytes 1179652 | tf_op jit(solution)/shard_map/while
  192.7 3.8 %copy-start.1 = (f32[2,768,768]{2,1,0:T(8,128)S(1)}, f32[2,768,768]{2,1,0:T(8,128)}, u32[]{:S(2)}) copy-start(f32[2,768,768]{2,1,0:T(8,128)} %get-tuple-element.517) | copy-start | bytes 14155780 | tf_op jit(solution)/shard_map/while
  192.7 3.8 %copy-start.3 = (bf16[768,256]{0,1:T(8,128)(2,1)S(1)}, bf16[768,256]{0,1:T(8,128)(2,1)}, u32[]{:S(2)}) copy-start(bf16[768,256]{0,1:T(8,128)(2,1)} %get-tuple-element.519) | copy-start | bytes 1179652 | tf_op jit(solution)/shard_map/while
  200.4 2.6 %copy-start.4 = (f32[2,256,128]{2,1,0:T(8,128)S(1)}, f32[2,256,128]{2,1,0:T(8,128)}, u32[]{:S(2)}) copy-start(f32[2,256,128]{2,1,0:T(8,128)} %custom-call.5) | copy-start | bytes 786436
  200.4 2.6 %copy-start.5 = (bf16[64,2,4,128]{3,2,0,1:T(4,128)(2,1)S(1)}, bf16[64,2,4,128]{3,2,0,1:T(4,128)(2,1)}, u32[]{:S(2)}) copy-start(bf16[64,2,4,128]{3,2,0,1:T(4,128)(2,1)} %copy.47) | copy-start | bytes 393220
  205.7 1.9 copy-start.2
  210.9 1.9 copy-start.2
Sparse Core Ops, SparseCore 0:
  9.6 39.7 all-gather.4
  53.4 45.2 all-gather.8
  101.2 44.5 reduce-scatter.1
  147.2 27.1 all-gather.6
